TPU v7x, 32 devices: a whole 2x2x4 slice. The times are simulated.
32 devices in a mesh: blk: 8 (over y, x, core), wide: 4 (over z).
Axes of the slice: x: 2, y: 2, z: 4, core: 2. Of those that a mesh axis runs over, the one named last changes fastest.
Arguments:
- points: bfloat16 [8192, 32], P(('blk', 'wide')), may hold values from -6 to 6
- inv_length: float32 [32], replicated, may hold values from 0.2 to 0.7
- noise_var: float32 [], replicated, may hold values from 0.1 to 1
- solution: float32 [8192, 128], P(('blk', 'wide')), may hold values from -6 to 6
- residual: float32 [8192, 128], P(('blk', 'wide')), may hold values from -6 to 6
- direction: float32 [8192, 128], P(('blk', 'wide')), may hold values from -6 to 6
Outputs:
- new_solution: float32 [8192, 128], P(('blk', 'wide'))
- new_residual: float32 [8192, 128], P(('blk', 'wide'))
- new_direction: float32 [8192, 128], P(('blk', 'wide'))
All inputs are finite; a program needn't handle non-finite values.
Results may differ from a plain program's by a relative error of at most 0.01.
Values may be sent and summed in bfloat16 or wider, within the bound.
A program may use at most 64 MiB of HBM per device.

v0:
```python
import jax
import jax.numpy as jnp
from jax import lax
from jax.sharding import PartitionSpec as P


def shifted(x, axis, by):
    count = lax.axis_size(axis)
    return lax.ppermute(x, axis, [(i, (i + by) % count) for i in range(count)])


def squares_of(values):
    wide_values = values.astype(jnp.float32)
    return jnp.sum(wide_values * wide_values, axis=1)


def kernel_tile(rows_x, rows_sq, cols_x, cols_sq):
    inner_prod = lax.dot_general(
        rows_x, cols_x, (((1,), (1,)), ((), ())), preferred_element_type=jnp.float32
    )
    dist_sq = jnp.maximum(rows_sq[:, None] + cols_sq[None, :] - 2.0 * inner_prod, 0.0)
    radius = jnp.sqrt(5.0 * dist_sq)
    return ((1.0 + radius + radius * radius / 3.0) * jnp.exp(-radius)).astype(jnp.bfloat16)


def on_device(points, inv_length, noise_var, solution, residual, direction):
    scaled = (points.astype(jnp.float32) * inv_length).astype(jnp.bfloat16)
    low_dir = direction.astype(jnp.bfloat16)
    own_sq = squares_of(scaled)
    block_x, block_p = (
        lax.all_gather(scaled, "wide", axis=0, tiled=True),
        lax.all_gather(low_dir, "wide", axis=0, tiled=True),
    )
    block_sq = squares_of(block_x)
    cycle_size = lax.axis_size("blk")
    row_sums = jnp.dot(
        kernel_tile(block_x, block_sq, scaled, own_sq), low_dir, preferred_element_type=jnp.float32
    )

    def direct_turn(counter, carried):
        piece_x, piece_p, row_total = carried
        piece_x, piece_p = shifted((piece_x, piece_p), "blk", 1)
        kernel_block = kernel_tile(block_x, block_sq, piece_x, squares_of(piece_x))
        row_total = row_total + jnp.dot(kernel_block, piece_p, preferred_element_type=jnp.float32)
        return (piece_x, piece_p, row_total)

    result = lax.fori_loop(0, cycle_size - 1, direct_turn, (scaled, low_dir, row_sums))
    own_image = lax.psum_scatter(result[2], "wide", scatter_dimension=0, tiled=True)
    kernel_image = own_image + noise_var * direction
    old_norm, curvature, cross_term, image_norm = lax.psum(
        (
            jnp.sum(residual * residual, axis=0),
            jnp.sum(direction * kernel_image, axis=0),
            jnp.sum(residual * kernel_image, axis=0),
            jnp.sum(kernel_image * kernel_image, axis=0),
        ),
        ("blk", "wide"),
    )
    step_length = old_norm / curvature
    new_residual = residual - step_length * kernel_image
    new_norm = old_norm - 2.0 * step_length * cross_term + step_length * step_length * image_norm
    new_solution = solution + step_length * direction
    new_direction = new_residual + new_norm / old_norm * direction
    return (new_solution, new_residual, new_direction)


def solution(mesh):
    return jax.shard_map(
        on_device,
        mesh=mesh,
        in_specs=(
            P(("blk", "wide"), None),
            P(),
            P(),
            P(("blk", "wide"), None),
            P(("blk", "wide"), None),
            P(("blk", "wide"), None),
        ),
        out_specs=(P(("blk", "wide"), None), P(("blk", "wide"), None), P(("blk", "wide"), None)),
        check_vma=False,
    )
```

profile of v0, /device:TPU:0, one launch (start us, length us, event | category | flops | bytes accessed | tf_op | source)
XLA Modules:
  0.0 140.3 jit_solution(16337664160268755583)
XLA Ops:
  7.2 0.8 copy.9
  8.2 15.7 %all_gather.3 = bf16[1024,32]{1,0:T(8,128)(2,1)S(1)} all-gather(bf16[256,32]{1,0:T(8,128)(2,1)S(1)} %get-tuple-element.102), channel_id=1, replica_groups=mesh['blk'=8,'wide'=4] {'wide'}, dimensions={0}, use_global_device_ids=true | all-gather | bytes 81920 | tf_op jit(solution)/shard_map/all_gather | solution.py:31
  24.1 0.7 copy-done
  24.8 0.9 fusion.16
  25.7 44.2 %while.14 = (s32[]{:T(128)}, bf16[256,32]{1,0:T(8,128)(2,1)S(1)}, bf16[256,128]{1,0:T(8,128)(2,1)S(1)}, f32[1024,128]{1,0:T(8,128)S(1)}, f32[1024]{0:T(1024)S(1)}, /*index=5*/bf16[1024,32]{1,0:T(8,128)(2,1)S(1)}, s32[]{:T(128)}) while((s32[]{:T(128)}, bf16[256,32]{1,0:T(8,128)(2,1)S(1)}, bf16[256,128]{1,0:T(8,128)(2,1)S(1)}, ...), condition=%wide.region_6.0_spmd, body=%wide.region_4.6_spmd.sunk | while | flops 87187200 | bytes 1710237 | solution.py:47
  25.8 1.6 %collective-permute-start.1 = (bf16[256,128]{1,0:T(8,128)(2,1)S(1)}, bf16[256,128]{1,0:T(8,128)(2,1)S(1)}, u32[]{:S(2)}, u32[]{:S(2)}) collective-permute-start(bf16[256,128]{1,0:T(8,128)(2,1)S(1)} %get-tuple-element.110), channel_id=1, source_target_pairs={{0,4},{4,8},{8,12},{12,16},{16,20},{20,24},{24,28},{28,0},{1,5},{5... | collective-permute-start | bytes 196616 | tf_op jit(solution)/shard_map/while/body/eval_jaxpr/ppermute | solution.py:9
  27.4 3.0 %collective-permute-done = bf16[256,32]{1,0:T(8,128)(2,1)S(1)} collective-permute-done((bf16[256,32]{1,0:T(8,128)(2,1)S(1)}, bf16[256,32]{1,0:T(8,128)(2,1)S(1)}, u32[]{:S(2)}, u32[]{:S(2)}) %collective-permute-start) | collective-permute-done | bytes 16416 | tf_op jit(solution)/shard_map/while/body/eval_jaxpr/ppermute | solution.py:9
  30.5 0.6 collective-permute-done.1
  31.0 1.0 convolution_add_fusion.2
  32.1 0.7 collective-permute-start.1
  32.8 3.9 %collective-permute-done = bf16[256,32]{1,0:T(8,128)(2,1)S(1)} collective-permute-done((bf16[256,32]{1,0:T(8,128)(2,1)S(1)}, bf16[256,32]{1,0:T(8,128)(2,1)S(1)}, u32[]{:S(2)}, u32[]{:S(2)}) %collective-permute-start) | collective-permute-done | bytes 16416 | tf_op jit(solution)/shard_map/while/body/eval_jaxpr/ppermute | solution.py:9
  36.8 0.6 collective-permute-done.1
  37.4 1.0 convolution_add_fusion.2
  38.4 4.5 %collective-permute-done = bf16[256,32]{1,0:T(8,128)(2,1)S(1)} collective-permute-done((bf16[256,32]{1,0:T(8,128)(2,1)S(1)}, bf16[256,32]{1,0:T(8,128)(2,1)S(1)}, u32[]{:S(2)}, u32[]{:S(2)}) %collective-permute-start) | collective-permute-done | bytes 16416 | tf_op jit(solution)/shard_map/while/body/eval_jaxpr/ppermute | solution.py:9
  43.1 0.6 collective-permute-done.1
  43.7 1.0 convolution_add_fusion.2
  44.7 4.5 %collective-permute-done = bf16[256,32]{1,0:T(8,128)(2,1)S(1)} collective-permute-done((bf16[256,32]{1,0:T(8,128)(2,1)S(1)}, bf16[256,32]{1,0:T(8,128)(2,1)S(1)}, u32[]{:S(2)}, u32[]{:S(2)}) %collective-permute-start) | collective-permute-done | bytes 16416 | tf_op jit(solution)/shard_map/while/body/eval_jaxpr/ppermute | solution.py:9
  49.4 0.6 collective-permute-done.1
  50.0 1.0 convolution_add_fusion.2
  51.1 4.5 %collective-permute-done = bf16[256,32]{1,0:T(8,128)(2,1)S(1)} collective-permute-done((bf16[256,32]{1,0:T(8,128)(2,1)S(1)}, bf16[256,32]{1,0:T(8,128)(2,1)S(1)}, u32[]{:S(2)}, u32[]{:S(2)}) %collective-permute-start) | collective-permute-done | bytes 16416 | tf_op jit(solution)/shard_map/while/body/eval_jaxpr/ppermute | solution.py:9
  55.7 0.6 collective-permute-done.1
  56.3 1.0 convolution_add_fusion.2
  57.4 4.5 %collective-permute-done = bf16[256,32]{1,0:T(8,128)(2,1)S(1)} collective-permute-done((bf16[256,32]{1,0:T(8,128)(2,1)S(1)}, bf16[256,32]{1,0:T(8,128)(2,1)S(1)}, u32[]{:S(2)}, u32[]{:S(2)}) %collective-permute-start) | collective-permute-done | bytes 16416 | tf_op jit(solution)/shard_map/while/body/eval_jaxpr/ppermute | solution.py:9
  62.6 1.0 convolution_add_fusion.2
  63.7 4.5 %collective-permute-done = bf16[256,32]{1,0:T(8,128)(2,1)S(1)} collective-permute-done((bf16[256,32]{1,0:T(8,128)(2,1)S(1)}, bf16[256,32]{1,0:T(8,128)(2,1)S(1)}, u32[]{:S(2)}, u32[]{:S(2)}) %collective-permute-start) | collective-permute-done | bytes 16416 | tf_op jit(solution)/shard_map/while/body/eval_jaxpr/ppermute | solution.py:9
  68.3 0.6 collective-permute-done.1
  68.9 1.0 convolution_add_fusion.2
  69.9 0.8 copy-done.1
  71.3 22.0 %reduce-scatter.2.cloned.1.call-done = f32[256,128]{1,0:T(8,128)} async-done(((f32[1024,128]{1,0:T(8,128)}), f32[256,128]{1,0:T(8,128)}) %reduce-scatter.2.cloned.1.call-update) | async-done | bytes 131088 | tf_op jit(solution)/shard_map/reduce_scatter | solution.py:48
  93.3 1.0 multiply_reduce_fusion.3
  94.3 38.4 %all-reduce = (f32[128]{0:T(128)S(1)}, f32[128]{0:T(128)S(1)}, f32[128]{0:T(128)S(1)}, f32[128]{0:T(128)S(1)}) all-reduce(f32[128]{0:T(128)S(1)} %get-tuple-element.39, f32[128]{0:T(128)S(1)} %get-tuple-element.38, f32[128]{0:T(128)S(1)} %get-tuple-element.37, ...), channel_id=1, replica_groups=mesh['blk'=8,'wide'=4] {'blk','wide'}, use_global_device_ids=true, to_apply=%region_1.0 | all-reduce | flops 512 | bytes 4096 | tf_op jit(solution)/shard_map/psum | solution.py:50
  132.7 0.8 multiply_add_fusion
  (48 shorter events, 2.6 us)
Async XLA Ops:
  7.2 0.9 copy-start.4
  7.2 86.1 %reduce-scatter.2.cloned.1.call-start = ((), (), s32[]{:S(2)}) async-start(), calls=%async_computation.1 | async-start | bytes 655360 | tf_op jit(solution)/shard_map/reduce_scatter | solution.py:48
  23.8 0.9 copy-start
  25.7 4.6 %collective-permute-start = (bf16[256,32]{1,0:T(8,128)(2,1)S(1)}, bf16[256,32]{1,0:T(8,128)(2,1)S(1)}, u32[]{:S(2)}, u32[]{:S(2)}) collective-permute-start(bf16[256,32]{1,0:T(8,128)(2,1)S(1)} %get-tuple-element.109), channel_id=1, source_target_pairs={{0,4},{4,8},{8,12},{12,16},{16,20},{20,24},{24,28},{28,0},{1,5},{5... | collective-permute-start | bytes 49160 | tf_op jit(solution)/shard_map/while/body/eval_jaxpr/ppermute | solution.py:9
  25.8 5.3 %collective-permute-start.1 = (bf16[256,128]{1,0:T(8,128)(2,1)S(1)}, bf16[256,128]{1,0:T(8,128)(2,1)S(1)}, u32[]{:S(2)}, u32[]{:S(2)}) collective-permute-start(bf16[256,128]{1,0:T(8,128)(2,1)S(1)} %get-tuple-element.110), channel_id=1, source_target_pairs={{0,4},{4,8},{8,12},{12,16},{16,20},{20,24},{24,28},{28,0},{1,5},{5... | collective-permute-start | bytes 196616 | tf_op jit(solution)/shard_map/while/body/eval_jaxpr/ppermute | solution.py:9
  32.0 4.6 %collective-permute-start = (bf16[256,32]{1,0:T(8,128)(2,1)S(1)}, bf16[256,32]{1,0:T(8,128)(2,1)S(1)}, u32[]{:S(2)}, u32[]{:S(2)}) collective-permute-start(bf16[256,32]{1,0:T(8,128)(2,1)S(1)} %get-tuple-element.109), channel_id=1, source_target_pairs={{0,4},{4,8},{8,12},{12,16},{16,20},{20,24},{24,28},{28,0},{1,5},{5... | collective-permute-start | bytes 49160 | tf_op jit(solution)/shard_map/while/body/eval_jaxpr/ppermute | solution.py:9
  32.1 5.3 %collective-permute-start.1 = (bf16[256,128]{1,0:T(8,128)(2,1)S(1)}, bf16[256,128]{1,0:T(8,128)(2,1)S(1)}, u32[]{:S(2)}, u32[]{:S(2)}) collective-permute-start(bf16[256,128]{1,0:T(8,128)(2,1)S(1)} %get-tuple-element.110), channel_id=1, source_target_pairs={{0,4},{4,8},{8,12},{12,16},{16,20},{20,24},{24,28},{28,0},{1,5},{5... | collective-permute-start | bytes 196616 | tf_op jit(solution)/shard_map/while/body/eval_jaxpr/ppermute | solution.py:9
  38.3 4.6 %collective-permute-start = (bf16[256,32]{1,0:T(8,128)(2,1)S(1)}, bf16[256,32]{1,0:T(8,128)(2,1)S(1)}, u32[]{:S(2)}, u32[]{:S(2)}) collective-permute-start(bf16[256,32]{1,0:T(8,128)(2,1)S(1)} %get-tuple-element.109), channel_id=1, source_target_pairs={{0,4},{4,8},{8,12},{12,16},{16,20},{20,24},{24,28},{28,0},{1,5},{5... | collective-permute-start | bytes 49160 | tf_op jit(solution)/shard_map/while/body/eval_jaxpr/ppermute | solution.py:9
  38.4 5.3 %collective-permute-start.1 = (bf16[256,128]{1,0:T(8,128)(2,1)S(1)}, bf16[256,128]{1,0:T(8,128)(2,1)S(1)}, u32[]{:S(2)}, u32[]{:S(2)}) collective-permute-start(bf16[256,128]{1,0:T(8,128)(2,1)S(1)} %get-tuple-element.110), channel_id=1, source_target_pairs={{0,4},{4,8},{8,12},{12,16},{16,20},{20,24},{24,28},{28,0},{1,5},{5... | collective-permute-start | bytes 196616 | tf_op jit(solution)/shard_map/while/body/eval_jaxpr/ppermute | solution.py:9
  44.6 4.6 %collective-permute-start = (bf16[256,32]{1,0:T(8,128)(2,1)S(1)}, bf16[256,32]{1,0:T(8,128)(2,1)S(1)}, u32[]{:S(2)}, u32[]{:S(2)}) collective-permute-start(bf16[256,32]{1,0:T(8,128)(2,1)S(1)} %get-tuple-element.109), channel_id=1, source_target_pairs={{0,4},{4,8},{8,12},{12,16},{16,20},{20,24},{24,28},{28,0},{1,5},{5... | collective-permute-start | bytes 49160 | tf_op jit(solution)/shard_map/while/body/eval_jaxpr/ppermute | solution.py:9
  44.7 5.3 %collective-permute-start.1 = (bf16[256,128]{1,0:T(8,128)(2,1)S(1)}, bf16[256,128]{1,0:T(8,128)(2,1)S(1)}, u32[]{:S(2)}, u32[]{:S(2)}) collective-permute-start(bf16[256,128]{1,0:T(8,128)(2,1)S(1)} %get-tuple-element.110), channel_id=1, source_target_pairs={{0,4},{4,8},{8,12},{12,16},{16,20},{20,24},{24,28},{28,0},{1,5},{5... | collective-permute-start | bytes 196616 | tf_op jit(solution)/shard_map/while/body/eval_jaxpr/ppermute | solution.py:9
  50.9 4.6 %collective-permute-start = (bf16[256,32]{1,0:T(8,128)(2,1)S(1)}, bf16[256,32]{1,0:T(8,128)(2,1)S(1)}, u32[]{:S(2)}, u32[]{:S(2)}) collective-permute-start(bf16[256,32]{1,0:T(8,128)(2,1)S(1)} %get-tuple-element.109), channel_id=1, source_target_pairs={{0,4},{4,8},{8,12},{12,16},{16,20},{20,24},{24,28},{28,0},{1,5},{5... | collective-permute-start | bytes 49160 | tf_op jit(solution)/shard_map/while/body/eval_jaxpr/ppermute | solution.py:9
  51.0 5.3 %collective-permute-start.1 = (bf16[256,128]{1,0:T(8,128)(2,1)S(1)}, bf16[256,128]{1,0:T(8,128)(2,1)S(1)}, u32[]{:S(2)}, u32[]{:S(2)}) collective-permute-start(bf16[256,128]{1,0:T(8,128)(2,1)S(1)} %get-tuple-element.110), channel_id=1, source_target_pairs={{0,4},{4,8},{8,12},{12,16},{16,20},{20,24},{24,28},{28,0},{1,5},{5... | collective-permute-start | bytes 196616 | tf_op jit(solution)/shard_map/while/body/eval_jaxpr/ppermute | solution.py:9
  57.2 4.6 %collective-permute-start = (bf16[256,32]{1,0:T(8,128)(2,1)S(1)}, bf16[256,32]{1,0:T(8,128)(2,1)S(1)}, u32[]{:S(2)}, u32[]{:S(2)}) collective-permute-start(bf16[256,32]{1,0:T(8,128)(2,1)S(1)} %get-tuple-element.109), channel_id=1, source_target_pairs={{0,4},{4,8},{8,12},{12,16},{16,20},{20,24},{24,28},{28,0},{1,5},{5... | collective-permute-start | bytes 49160 | tf_op jit(solution)/shard_map/while/body/eval_jaxpr/ppermute | solution.py:9
  57.3 5.3 %collective-permute-start.1 = (bf16[256,128]{1,0:T(8,128)(2,1)S(1)}, bf16[256,128]{1,0:T(8,128)(2,1)S(1)}, u32[]{:S(2)}, u32[]{:S(2)}) collective-permute-start(bf16[256,128]{1,0:T(8,128)(2,1)S(1)} %get-tuple-element.110), channel_id=1, source_target_pairs={{0,4},{4,8},{8,12},{12,16},{16,20},{20,24},{24,28},{28,0},{1,5},{5... | collective-permute-start | bytes 196616 | tf_op jit(solution)/shard_map/while/body/eval_jaxpr/ppermute | solution.py:9
  63.5 4.6 %collective-permute-start = (bf16[256,32]{1,0:T(8,128)(2,1)S(1)}, bf16[256,32]{1,0:T(8,128)(2,1)S(1)}, u32[]{:S(2)}, u32[]{:S(2)}) collective-permute-start(bf16[256,32]{1,0:T(8,128)(2,1)S(1)} %get-tuple-element.109), channel_id=1, source_target_pairs={{0,4},{4,8},{8,12},{12,16},{16,20},{20,24},{24,28},{28,0},{1,5},{5... | collective-permute-start | bytes 49160 | tf_op jit(solution)/shard_map/while/body/eval_jaxpr/ppermute | solution.py:9
  63.6 5.3 %collective-permute-start.1 = (bf16[256,128]{1,0:T(8,128)(2,1)S(1)}, bf16[256,128]{1,0:T(8,128)(2,1)S(1)}, u32[]{:S(2)}, u32[]{:S(2)}) collective-permute-start(bf16[256,128]{1,0:T(8,128)(2,1)S(1)} %get-tuple-element.110), channel_id=1, source_target_pairs={{0,4},{4,8},{8,12},{12,16},{16,20},{20,24},{24,28},{28,0},{1,5},{5... | collective-permute-start | bytes 196616 | tf_op jit(solution)/shard_map/while/body/eval_jaxpr/ppermute | solution.py:9
  69.8 0.8 copy-start.1
  69.8 23.4 %copy-start.2 = (f32[256,128]{1,0:T(8,128)S(1)}, f32[256,128]{1,0:T(8,128)}, u32[]{:S(2)}) copy-start(f32[256,128]{1,0:T(8,128)} %param.12) | copy-start | bytes 393220
  71.3 61.3 %copy-start.3 = (f32[256,128]{1,0:T(8,128)S(1)}, f32[256,128]{1,0:T(8,128)}, u32[]{:S(2)}) copy-start(f32[256,128]{1,0:T(8,128)} %param.11) | copy-start | bytes 393220
Sparse Core Ops, SparseCore 0:
  70.8 22.4 reduce-scatter.1
where the time goes:
time: 141 us; the launch traced here: 140 us
  waiting for transfers between devices  55.4 us (39%)
  blocking collectives  54 us (38%)
  between operations  14.7 us (10%)
  matrix products  7.59 us (5%)
  starting transfers between devices  3.02 us (2%)
  other arithmetic  2.87 us (2%)
  local copies, waits for them, and re-layouts  2.4 us (2%)
    psum x1, blocking collectives, on_device(): lax.psum((jnp.sum(residual * residual, axis=0), jnp.sum(direction * kerne...  38.4 us
    ppermute x14, waiting for transfers between devices, shifted(): return lax.ppermute(x, axis, [(i, (i + by) % count) for i in range(count)])  33.5 us
    reduce_scatter x1, waiting for transfers between devices, on_device(): lax.psum_scatter(result[2], 'wide', scatter_dimension=0, tiled=True)  22 us
    all_gather x1, blocking collectives, on_device(): lax.all_gather(scaled, 'wide', axis=0, tiled=True)  15.7 us
    dot_general x7, matrix products, direct_turn(): jnp.dot(kernel_block, piece_p, preferred_element_type=jnp.float32)  6.66 us
    ppermute x14, starting transfers between devices, shifted(): return lax.ppermute(x, axis, [(i, (i + by) % count) for i in range(count)])  2.98 us
  transfers between devices with their start and end apart: 15, of which 15 were waited for; matrix products, arithmetic and copies ran while one was open for 1% of the time, Pallas kernels for 0%

commit v1 on v0

--- a/solution.py
+++ b/solution.py
@@ -48,13 +48,16 @@
     own_image = lax.psum_scatter(result[2], "wide", scatter_dimension=0, tiled=True)
     kernel_image = own_image + noise_var * direction
     old_norm, curvature, cross_term, image_norm = lax.psum(
-        (
-            jnp.sum(residual * residual, axis=0),
-            jnp.sum(direction * kernel_image, axis=0),
-            jnp.sum(residual * kernel_image, axis=0),
-            jnp.sum(kernel_image * kernel_image, axis=0),
+        lax.psum(
+            (
+                jnp.sum(residual * residual, axis=0),
+                jnp.sum(direction * kernel_image, axis=0),
+                jnp.sum(residual * kernel_image, axis=0),
+                jnp.sum(kernel_image * kernel_image, axis=0),
+            ),
+            "wide",
         ),
-        ("blk", "wide"),
+        "blk",
     )
     step_length = old_norm / curvature
     new_residual = residual - step_length * kernel_image

time: 141 us -> 123 us (0.87)
  blocking collectives: 54 us -> 36.1 us
    psum x1, blocking collectives: 38.4 us -> 8.59 us  [on_device(): lax.psum((jnp.sum(residual * residual, axis=0), jnp.sum(direction * kerne...]
    psum x0 -> x1, blocking collectives: none -> 11.8 us  [on_device(): lax.psum(lax.psum((jnp.sum(residual * residual, axis=0), jnp.sum(directio...]
where the time goes in v1:
time: 123 us; the launch traced here: 122 us
  waiting for transfers between devices  55.4 us (45%)
  blocking collectives  36.1 us (29%)
  between operations  14.7 us (12%)
  matrix products  7.59 us (6%)
  starting transfers between devices  3.02 us (2%)
  other arithmetic  2.87 us (2%)
  local copies, waits for them, and re-layouts  2.4 us (2%)
    ppermute x14, waiting for transfers between devices, shifted(): return lax.ppermute(x, axis, [(i, (i + by) % count) for i in range(count)])  33.5 us
    reduce_scatter x1, waiting for transfers between devices, on_device(): lax.psum_scatter(result[2], 'wide', scatter_dimension=0, tiled=True)  22 us
    all_gather x1, blocking collectives, on_device(): lax.all_gather(scaled, 'wide', axis=0, tiled=True)  15.7 us
    psum x1, blocking collectives, on_device(): lax.psum(lax.psum((jnp.sum(residual * residual, axis=0), jnp.sum(directio...  11.8 us
    psum x1, blocking collectives, on_device(): lax.psum((jnp.sum(residual * residual, axis=0), jnp.sum(direction * kerne...  8.59 us
    dot_general x7, matrix products, direct_turn(): jnp.dot(kernel_block, piece_p, preferred_element_type=jnp.float32)  6.66 us
    ppermute x14, starting transfers between devices, shifted(): return lax.ppermute(x, axis, [(i, (i + by) % count) for i in range(count)])  2.98 us
  transfers between devices with their start and end apart: 15, of which 15 were waited for; matrix products, arithmetic and copies ran while one was open for 1% of the time, Pallas kernels for 0%

profile of v1, /device:TPU:0, one launch (start us, length us, event | category | flops | bytes accessed | tf_op | source)
XLA Modules:
  0.0 122.3 jit_solution(2700069527045883261)
XLA Ops:
  7.2 0.8 copy.9
  8.2 15.7 %all_gather.3 = bf16[1024,32]{1,0:T(8,128)(2,1)S(1)} all-gather(bf16[256,32]{1,0:T(8,128)(2,1)S(1)} %get-tuple-element.106), channel_id=1, replica_groups=mesh['blk'=8,'wide'=4] {'wide'}, dimensions={0}, use_global_device_ids=true | all-gather | bytes 81920 | tf_op jit(solution)/shard_map/all_gather | solution.py:31
  24.1 0.7 copy-done
  24.8 0.9 fusion.16
  25.7 44.2 %while.14 = (s32[]{:T(128)}, bf16[256,32]{1,0:T(8,128)(2,1)S(1)}, bf16[256,128]{1,0:T(8,128)(2,1)S(1)}, f32[1024,128]{1,0:T(8,128)S(1)}, f32[1024]{0:T(1024)S(1)}, /*index=5*/bf16[1024,32]{1,0:T(8,128)(2,1)S(1)}, s32[]{:T(128)}) while((s32[]{:T(128)}, bf16[256,32]{1,0:T(8,128)(2,1)S(1)}, bf16[256,128]{1,0:T(8,128)(2,1)S(1)}, ...), condition=%wide.region_7.0_spmd, body=%wide.region_5.7_spmd.sunk | while | flops 87187200 | bytes 1710237 | solution.py:47
  25.8 1.6 %collective-permute-start.1 = (bf16[256,128]{1,0:T(8,128)(2,1)S(1)}, bf16[256,128]{1,0:T(8,128)(2,1)S(1)}, u32[]{:S(2)}, u32[]{:S(2)}) collective-permute-start(bf16[256,128]{1,0:T(8,128)(2,1)S(1)} %get-tuple-element.114), channel_id=1, source_target_pairs={{0,4},{4,8},{8,12},{12,16},{16,20},{20,24},{24,28},{28,0},{1,5},{5... | collective-permute-start | bytes 196616 | tf_op jit(solution)/shard_map/while/body/eval_jaxpr/ppermute | solution.py:9
  27.4 3.0 %collective-permute-done = bf16[256,32]{1,0:T(8,128)(2,1)S(1)} collective-permute-done((bf16[256,32]{1,0:T(8,128)(2,1)S(1)}, bf16[256,32]{1,0:T(8,128)(2,1)S(1)}, u32[]{:S(2)}, u32[]{:S(2)}) %collective-permute-start) | collective-permute-done | bytes 16416 | tf_op jit(solution)/shard_map/while/body/eval_jaxpr/ppermute | solution.py:9
  30.5 0.6 collective-permute-done.1
  31.0 1.0 convolution_add_fusion.2
  32.1 0.7 collective-permute-start.1
  32.8 3.9 %collective-permute-done = bf16[256,32]{1,0:T(8,128)(2,1)S(1)} collective-permute-done((bf16[256,32]{1,0:T(8,128)(2,1)S(1)}, bf16[256,32]{1,0:T(8,128)(2,1)S(1)}, u32[]{:S(2)}, u32[]{:S(2)}) %collective-permute-start) | collective-permute-done | bytes 16416 | tf_op jit(solution)/shard_map/while/body/eval_jaxpr/ppermute | solution.py:9
  36.8 0.6 collective-permute-done.1
  37.4 1.0 convolution_add_fusion.2
  38.4 4.5 %collective-permute-done = bf16[256,32]{1,0:T(8,128)(2,1)S(1)} collective-permute-done((bf16[256,32]{1,0:T(8,128)(2,1)S(1)}, bf16[256,32]{1,0:T(8,128)(2,1)S(1)}, u32[]{:S(2)}, u32[]{:S(2)}) %collective-permute-start) | collective-permute-done | bytes 16416 | tf_op jit(solution)/shard_map/while/body/eval_jaxpr/ppermute | solution.py:9
  43.1 0.6 collective-permute-done.1
  43.7 1.0 convolution_add_fusion.2
  44.7 4.5 %collective-permute-done = bf16[256,32]{1,0:T(8,128)(2,1)S(1)} collective-permute-done((bf16[256,32]{1,0:T(8,128)(2,1)S(1)}, bf16[256,32]{1,0:T(8,128)(2,1)S(1)}, u32[]{:S(2)}, u32[]{:S(2)}) %collective-permute-start) | collective-permute-done | bytes 16416 | tf_op jit(solution)/shard_map/while/body/eval_jaxpr/ppermute | solution.py:9
  50.0 1.0 convolution_add_fusion.2
  51.1 4.5 %collective-permute-done = bf16[256,32]{1,0:T(8,128)(2,1)S(1)} collective-permute-done((bf16[256,32]{1,0:T(8,128)(2,1)S(1)}, bf16[256,32]{1,0:T(8,128)(2,1)S(1)}, u32[]{:S(2)}, u32[]{:S(2)}) %collective-permute-start) | collective-permute-done | bytes 16416 | tf_op jit(solution)/shard_map/while/body/eval_jaxpr/ppermute | solution.py:9
  55.7 0.6 collective-permute-done.1
  56.3 1.0 convolution_add_fusion.2
  57.4 4.5 %collective-permute-done = bf16[256,32]{1,0:T(8,128)(2,1)S(1)} collective-permute-done((bf16[256,32]{1,0:T(8,128)(2,1)S(1)}, bf16[256,32]{1,0:T(8,128)(2,1)S(1)}, u32[]{:S(2)}, u32[]{:S(2)}) %collective-permute-start) | collective-permute-done | bytes 16416 | tf_op jit(solution)/shard_map/while/body/eval_jaxpr/ppermute | solution.py:9
  62.6 1.0 convolution_add_fusion.2
  63.7 4.5 %collective-permute-done = bf16[256,32]{1,0:T(8,128)(2,1)S(1)} collective-permute-done((bf16[256,32]{1,0:T(8,128)(2,1)S(1)}, bf16[256,32]{1,0:T(8,128)(2,1)S(1)}, u32[]{:S(2)}, u32[]{:S(2)}) %collective-permute-start) | collective-permute-done | bytes 16416 | tf_op jit(solution)/shard_map/while/body/eval_jaxpr/ppermute | solution.py:9
  68.3 0.6 collective-permute-done.1
  68.9 1.0 convolution_add_fusion.2
  69.9 0.8 copy-done.1
  71.3 22.0 %reduce-scatter.2.cloned.1.call-done = f32[256,128]{1,0:T(8,128)} async-done(((f32[1024,128]{1,0:T(8,128)}), f32[256,128]{1,0:T(8,128)}) %reduce-scatter.2.cloned.1.call-update) | async-done | bytes 131088 | tf_op jit(solution)/shard_map/reduce_scatter | solution.py:48
  93.3 1.0 multiply_reduce_fusion.3
  94.3 8.6 %all-reduce.1 = (f32[128]{0:T(128)S(1)}, f32[128]{0:T(128)S(1)}, f32[128]{0:T(128)S(1)}, f32[128]{0:T(128)S(1)}) all-reduce(f32[128]{0:T(128)S(1)} %get-tuple-element.39, f32[128]{0:T(128)S(1)} %get-tuple-element.38, f32[128]{0:T(128)S(1)} %get-tuple-element.37, f32[128]{0:T(128)S(1)} %get-tuple-element.36), channel_id=1, replica_groups=mesh['blk'=8,'wide'=4] {'wide'}, use_global_device_ids=true, to_apply=%region_1.0 | all-reduce | flops 512 | bytes 4096 | tf_op jit(solution)/shard_map/psum | solution.py:51
  102.9 11.8 %all-reduce = (f32[128]{0:T(128)S(1)}, f32[128]{0:T(128)S(1)}, f32[128]{0:T(128)S(1)}, f32[128]{0:T(128)S(1)}) all-reduce(f32[128]{0:T(128)S(1)} %get-tuple-element.56, f32[128]{0:T(128)S(1)} %get-tuple-element.57, f32[128]{0:T(128)S(1)} %get-tuple-element.58, f32[128]{0:T(128)S(1)} %get-tuple-element.59), channel_id=1, replica_groups=mesh['blk'=8,'wide'=4] {'blk'}, use_global_device_ids=true, to_apply=%region_2.3 | all-reduce | flops 512 | bytes 4096 | tf_op jit(solution)/shard_map/psum | solution.py:50
  114.7 0.8 multiply_add_fusion
  (49 shorter events, 3.1 us)
Async XLA Ops:
  7.2 0.9 copy-start.4
  7.2 86.1 %reduce-scatter.2.cloned.1.call-start = ((), (), s32[]{:S(2)}) async-start(), calls=%async_computation.1 | async-start | bytes 655360 | tf_op jit(solution)/shard_map/reduce_scatter | solution.py:48
  23.8 0.9 copy-start
  25.7 4.6 %collective-permute-start = (bf16[256,32]{1,0:T(8,128)(2,1)S(1)}, bf16[256,32]{1,0:T(8,128)(2,1)S(1)}, u32[]{:S(2)}, u32[]{:S(2)}) collective-permute-start(bf16[256,32]{1,0:T(8,128)(2,1)S(1)} %get-tuple-element.113), channel_id=1, source_target_pairs={{0,4},{4,8},{8,12},{12,16},{16,20},{20,24},{24,28},{28,0},{1,5},{5... | collective-permute-start | bytes 49160 | tf_op jit(solution)/shard_map/while/body/eval_jaxpr/ppermute | solution.py:9
  25.8 5.3 %collective-permute-start.1 = (bf16[256,128]{1,0:T(8,128)(2,1)S(1)}, bf16[256,128]{1,0:T(8,128)(2,1)S(1)}, u32[]{:S(2)}, u32[]{:S(2)}) collective-permute-start(bf16[256,128]{1,0:T(8,128)(2,1)S(1)} %get-tuple-element.114), channel_id=1, source_target_pairs={{0,4},{4,8},{8,12},{12,16},{16,20},{20,24},{24,28},{28,0},{1,5},{5... | collective-permute-start | bytes 196616 | tf_op jit(solution)/shard_map/while/body/eval_jaxpr/ppermute | solution.py:9
  32.0 4.6 %collective-permute-start = (bf16[256,32]{1,0:T(8,128)(2,1)S(1)}, bf16[256,32]{1,0:T(8,128)(2,1)S(1)}, u32[]{:S(2)}, u32[]{:S(2)}) collective-permute-start(bf16[256,32]{1,0:T(8,128)(2,1)S(1)} %get-tuple-element.113), channel_id=1, source_target_pairs={{0,4},{4,8},{8,12},{12,16},{16,20},{20,24},{24,28},{28,0},{1,5},{5... | collective-permute-start | bytes 49160 | tf_op jit(solution)/shard_map/while/body/eval_jaxpr/ppermute | solution.py:9
  32.1 5.3 %collective-permute-start.1 = (bf16[256,128]{1,0:T(8,128)(2,1)S(1)}, bf16[256,128]{1,0:T(8,128)(2,1)S(1)}, u32[]{:S(2)}, u32[]{:S(2)}) collective-permute-start(bf16[256,128]{1,0:T(8,128)(2,1)S(1)} %get-tuple-element.114), channel_id=1, source_target_pairs={{0,4},{4,8},{8,12},{12,16},{16,20},{20,24},{24,28},{28,0},{1,5},{5... | collective-permute-start | bytes 196616 | tf_op jit(solution)/shard_map/while/body/eval_jaxpr/ppermute | solution.py:9
  38.3 4.6 %collective-permute-start = (bf16[256,32]{1,0:T(8,128)(2,1)S(1)}, bf16[256,32]{1,0:T(8,128)(2,1)S(1)}, u32[]{:S(2)}, u32[]{:S(2)}) collective-permute-start(bf16[256,32]{1,0:T(8,128)(2,1)S(1)} %get-tuple-element.113), channel_id=1, source_target_pairs={{0,4},{4,8},{8,12},{12,16},{16,20},{20,24},{24,28},{28,0},{1,5},{5... | collective-permute-start | bytes 49160 | tf_op jit(solution)/shard_map/while/body/eval_jaxpr/ppermute | solution.py:9
  38.4 5.3 %collective-permute-start.1 = (bf16[256,128]{1,0:T(8,128)(2,1)S(1)}, bf16[256,128]{1,0:T(8,128)(2,1)S(1)}, u32[]{:S(2)}, u32[]{:S(2)}) collective-permute-start(bf16[256,128]{1,0:T(8,128)(2,1)S(1)} %get-tuple-element.114), channel_id=1, source_target_pairs={{0,4},{4,8},{8,12},{12,16},{16,20},{20,24},{24,28},{28,0},{1,5},{5... | collective-permute-start | bytes 196616 | tf_op jit(solution)/shard_map/while/body/eval_jaxpr/ppermute | solution.py:9
  44.6 4.6 %collective-permute-start = (bf16[256,32]{1,0:T(8,128)(2,1)S(1)}, bf16[256,32]{1,0:T(8,128)(2,1)S(1)}, u32[]{:S(2)}, u32[]{:S(2)}) collective-permute-start(bf16[256,32]{1,0:T(8,128)(2,1)S(1)} %get-tuple-element.113), channel_id=1, source_target_pairs={{0,4},{4,8},{8,12},{12,16},{16,20},{20,24},{24,28},{28,0},{1,5},{5... | collective-permute-start | bytes 49160 | tf_op jit(solution)/shard_map/while/body/eval_jaxpr/ppermute | solution.py:9
  44.7 5.3 %collective-permute-start.1 = (bf16[256,128]{1,0:T(8,128)(2,1)S(1)}, bf16[256,128]{1,0:T(8,128)(2,1)S(1)}, u32[]{:S(2)}, u32[]{:S(2)}) collective-permute-start(bf16[256,128]{1,0:T(8,128)(2,1)S(1)} %get-tuple-element.114), channel_id=1, source_target_pairs={{0,4},{4,8},{8,12},{12,16},{16,20},{20,24},{24,28},{28,0},{1,5},{5... | collective-permute-start | bytes 196616 | tf_op jit(solution)/shard_map/while/body/eval_jaxpr/ppermute | solution.py:9
  50.9 4.6 %collective-permute-start = (bf16[256,32]{1,0:T(8,128)(2,1)S(1)}, bf16[256,32]{1,0:T(8,128)(2,1)S(1)}, u32[]{:S(2)}, u32[]{:S(2)}) collective-permute-start(bf16[256,32]{1,0:T(8,128)(2,1)S(1)} %get-tuple-element.113), channel_id=1, source_target_pairs={{0,4},{4,8},{8,12},{12,16},{16,20},{20,24},{24,28},{28,0},{1,5},{5... | collective-permute-start | bytes 49160 | tf_op jit(solution)/shard_map/while/body/eval_jaxpr/ppermute | solution.py:9
  51.0 5.3 %collective-permute-start.1 = (bf16[256,128]{1,0:T(8,128)(2,1)S(1)}, bf16[256,128]{1,0:T(8,128)(2,1)S(1)}, u32[]{:S(2)}, u32[]{:S(2)}) collective-permute-start(bf16[256,128]{1,0:T(8,128)(2,1)S(1)} %get-tuple-element.114), channel_id=1, source_target_pairs={{0,4},{4,8},{8,12},{12,16},{16,20},{20,24},{24,28},{28,0},{1,5},{5... | collective-permute-start | bytes 196616 | tf_op jit(solution)/shard_map/while/body/eval_jaxpr/ppermute | solution.py:9
  57.2 4.6 %collective-permute-start = (bf16[256,32]{1,0:T(8,128)(2,1)S(1)}, bf16[256,32]{1,0:T(8,128)(2,1)S(1)}, u32[]{:S(2)}, u32[]{:S(2)}) collective-permute-start(bf16[256,32]{1,0:T(8,128)(2,1)S(1)} %get-tuple-element.113), channel_id=1, source_target_pairs={{0,4},{4,8},{8,12},{12,16},{16,20},{20,24},{24,28},{28,0},{1,5},{5... | collective-permute-start | bytes 49160 | tf_op jit(solution)/shard_map/while/body/eval_jaxpr/ppermute | solution.py:9
  57.3 5.3 %collective-permute-start.1 = (bf16[256,128]{1,0:T(8,128)(2,1)S(1)}, bf16[256,128]{1,0:T(8,128)(2,1)S(1)}, u32[]{:S(2)}, u32[]{:S(2)}) collective-permute-start(bf16[256,128]{1,0:T(8,128)(2,1)S(1)} %get-tuple-element.114), channel_id=1, source_target_pairs={{0,4},{4,8},{8,12},{12,16},{16,20},{20,24},{24,28},{28,0},{1,5},{5... | collective-permute-start | bytes 196616 | tf_op jit(solution)/shard_map/while/body/eval_jaxpr/ppermute | solution.py:9
  63.5 4.6 %collective-permute-start = (bf16[256,32]{1,0:T(8,128)(2,1)S(1)}, bf16[256,32]{1,0:T(8,128)(2,1)S(1)}, u32[]{:S(2)}, u32[]{:S(2)}) collective-permute-start(bf16[256,32]{1,0:T(8,128)(2,1)S(1)} %get-tuple-element.113), channel_id=1, source_target_pairs={{0,4},{4,8},{8,12},{12,16},{16,20},{20,24},{24,28},{28,0},{1,5},{5... | collective-permute-start | bytes 49160 | tf_op jit(solution)/shard_map/while/body/eval_jaxpr/ppermute | solution.py:9
  63.6 5.3 %collective-permute-start.1 = (bf16[256,128]{1,0:T(8,128)(2,1)S(1)}, bf16[256,128]{1,0:T(8,128)(2,1)S(1)}, u32[]{:S(2)}, u32[]{:S(2)}) collective-permute-start(bf16[256,128]{1,0:T(8,128)(2,1)S(1)} %get-tuple-element.114), channel_id=1, source_target_pairs={{0,4},{4,8},{8,12},{12,16},{16,20},{20,24},{24,28},{28,0},{1,5},{5... | collective-permute-start | bytes 196616 | tf_op jit(solution)/shard_map/while/body/eval_jaxpr/ppermute | solution.py:9
  69.8 0.8 copy-start.1
  69.8 23.4 %copy-start.2 = (f32[256,128]{1,0:T(8,128)S(1)}, f32[256,128]{1,0:T(8,128)}, u32[]{:S(2)}) copy-start(f32[256,128]{1,0:T(8,128)} %param.12) | copy-start | bytes 393220
  71.3 43.4 %copy-start.3 = (f32[256,128]{1,0:T(8,128)S(1)}, f32[256,128]{1,0:T(8,128)}, u32[]{:S(2)}) copy-start(f32[256,128]{1,0:T(8,128)} %param.11) | copy-start | bytes 393220
Sparse Core Ops, SparseCore 0:
  70.8 22.4 reduce-scatter.1
